TPU v7x, 128 devices: a whole 4x4x4 slice. The times are simulated.
128 devices in a mesh: expert: 8 (over x, core), tile: 16 (over z, y).
Axes of the slice: x: 4, y: 4, z: 4, core: 2. Of those that a mesh axis runs over, the one named last changes fastest.
Arguments:
- weight: bfloat16 [8, 2048, 8192], P('expert', None, 'tile'), may hold values from -6 to 6
- grad: bfloat16 [8, 2048, 8192], P('expert', None, 'tile'), may hold values from -24 to 24, as said below
- first_moment: float32 [8, 2048, 8192], P('expert', None, 'tile'), may hold values from -6 to 6
- second_moment: float32 [8, 2048, 8192], P('expert', None, 'tile'), may hold values from 0.25 to 4
- left_basis: bfloat16 [8, 1024, 2048], P('expert', None, 'tile'), may hold values from -1 to 1, as said below
- right_basis: bfloat16 [8, 1024, 8192], P('expert', None, 'tile'), may hold values from -1 to 1, as said below
Outputs:
- new_weight: bfloat16 [8, 2048, 8192], P('expert', None, 'tile')
- new_first: float32 [8, 2048, 8192], P('expert', None, 'tile')
- new_second: float32 [8, 2048, 8192], P('expert', None, 'tile')
Inputs may be any that keep to these rules, and one draw needn't show every extreme that they name: `grad`: scaled values. `left_basis`: every diagonal block is orthogonal before rounding to bfloat16. `right_basis`: every diagonal block is orthogonal before rounding to bfloat16.
All inputs are finite; a program needn't handle non-finite values.
Results may differ from a plain program's by a relative error of at most 0.0045.
Values may be sent and summed in bfloat16 or wider, within the bound.
No kernel may reach another device: no remote copies, remote signals or barrier semaphores. Data moves between devices by JAX's collectives and lax.ppermute only.
A program may use at most 128 MiB of HBM per device.

v0:
```python
import jax
import jax.numpy as jnp
from jax import lax
from jax.sharding import Mesh
from jax.sharding import PartitionSpec as P

TILE = ("tile_0", "tile_1")
EXPERT_TILE = ("expert_0", "expert_1", "tile_0", "tile_1")
EXPERT = ("expert_0", "expert_1")
beta_one = 0.9
beta_two = 0.95
epsilon = 1e-08
learn_rate = 0.25
decay_rate = 0.1


def one_axis_at_a_time(value, axes):
    for axis in axes:
        value = lax.psum(value, axis)
    return value


def swapped(value, axis, distance):
    mask = 2**distance
    pairs = [(source, source ^ mask) for source in range(lax.axis_size(axis))]
    return lax.ppermute(value, axis, pairs)


def doubling(items, position, send):
    other = send(items, 0)
    lower = position >> 0 & 1 == 0
    items = jnp.where(
        lower, jnp.concatenate((items, other), axis=2), jnp.concatenate((other, items), axis=2)
    )
    return items


def on_device(weight, grad, first_moment, second_moment, left_basis, right_basis):
    experts, rows, width = grad.shape
    block = right_basis.shape[1]
    group = block // width
    levels = group.bit_length() - 1
    position = lax.axis_index(TILE) % group
    left_count = rows // block
    local_total = jnp.sum(jnp.square(grad.astype(jnp.float32)))
    total = one_axis_at_a_time(local_total, EXPERT_TILE)
    count = experts * lax.axis_size(EXPERT) * rows * width * lax.axis_size(TILE)
    clip = 1.0 / jnp.maximum(1.0, jnp.sqrt(total / count))
    whole_left = lax.all_gather(left_basis, TILE, axis=2, tiled=True)
    left4 = whole_left.reshape(experts, block, left_count, block)
    grad4 = grad.reshape(experts, left_count, block, width)
    rotated_left = jnp.einsum("ekbi,ebkw->ebiw", left4, grad4, preferred_element_type=jnp.float32)
    rotated_left = rotated_left.reshape(experts, rows, width).astype(jnp.bfloat16)

    def send_rows(items, bit):
        return swapped(items, TILE, bit)

    left_block = doubling(rotated_left, position, send_rows)
    rotated = jnp.einsum(
        "edk,ekj->edj", left_block, right_basis, preferred_element_type=jnp.float32
    )
    clipped = clip * rotated
    new_first = beta_one * first_moment + (1.0 - beta_one) * clipped
    new_second = beta_two * second_moment + (1.0 - beta_two) * clipped * clipped
    update = (new_first / (jnp.sqrt(new_second) + epsilon)).astype(jnp.bfloat16)
    partial_term = jnp.einsum(
        "edj,ekj->edk", update, right_basis, preferred_element_type=jnp.float32
    )
    for bit in reversed(range(levels)):
        half = partial_term.shape[2] // 2
        first_half = partial_term[:, :, :half]
        second_half = partial_term[:, :, half:]
        upper = position >> bit & 1 == 1
        keeping = jnp.where(upper, second_half, first_half)
        sending = jnp.where(upper, first_half, second_half)
        partial_term = keeping + swapped(sending.astype(jnp.bfloat16), TILE, bit).astype(
            sending.dtype
        )
    back_right = partial_term.astype(jnp.bfloat16)
    back4 = back_right.reshape(experts, left_count, block, width)
    back = jnp.einsum("ekbi,ebiw->ebkw", left4, back4, preferred_element_type=jnp.float32).reshape(
        experts, rows, width
    )
    weight32 = weight.astype(jnp.float32)
    new_weight = (weight32 - learn_rate * (back + decay_rate * weight32)).astype(jnp.bfloat16)
    return (new_weight, new_first, new_second)


def solution(mesh):
    finer = Mesh(mesh.devices.reshape(4, 2, 4, 4), ("expert_0", "expert_1", "tile_0", "tile_1"))
    in_specs = (
        P(EXPERT, None, TILE),
        P(EXPERT, None, TILE),
        P(EXPERT, None, TILE),
        P(EXPERT, None, TILE),
        P(EXPERT, None, TILE),
        P(EXPERT, None, TILE),
    )
    out_specs = (P(EXPERT, None, TILE), P(EXPERT, None, TILE), P(EXPERT, None, TILE))
    return jax.shard_map(
        on_device, mesh=finer, in_specs=in_specs, out_specs=out_specs, check_vma=False
    )
```

profile of v0, /device:TPU:0, one launch (start us, length us, event | category | flops | bytes accessed | tf_op | source)
XLA Modules:
  0.0 212.0 jit_solution(10057856764942879282)
XLA Ops:
  7.2 0.0 copy-start
  7.2 0.0 all-gather.2.cloned.1.call-start
  7.2 0.7 all-gather.2.cloned.1.call-update
  7.9 61.7 %all-gather.2.cloned.1.call-done = bf16[1,1024,2048]{2,1,0:T(8,128)(2,1)} async-done(((bf16[1,1024,128]{2,1,0:T(8,128)(2,1)}), bf16[1,1024,2048]{2,1,0:T(8,128)(2,1)}) %all-gather.2.cloned.1.call-update) | async-done | bytes 4194320 | tf_op jit(solution)/shard_map/all_gather | solution.py:49
  69.6 6.4 %copy.12 = bf16[1,1024,2048]{1,2,0:T(8,128)(2,1)} copy(bf16[1,1024,2048]{2,1,0:T(8,128)(2,1)} %all-gather.2.cloned.1.call-done) | data formatting | bytes 8388608 | tf_op jit(solution)/shard_map/all_gather | solution.py:49
  76.0 5.8 %convolution_convert_fusion = bf16[2,1024,512]{2,1,0:T(8,128)(2,1)} fusion(bf16[1024,2,1024]{0,2,1:T(8,128)(2,1)} %bitcast.34, bf16[2,1024,512]{2,1,0:T(8,128)(2,1)S(1)} %bitcast.37), kind=kOutput, calls=%fused_computation.24 | convolution fusion | flops 2148532224 | bytes 8388608 | tf_op jit(solution)/shard_map/ekbi,ebkw->ebiw/dot_general | solution.py:52
  81.8 1.2 collective-permute-start
  83.0 1.7 multiply_reduce_fusion
  84.7 11.0 %psum.28 = f32[]{:T(128)} all-reduce(f32[]{:T(128)} %multiply_reduce_fusion), channel_id=1, replica_groups=mesh['expert_0'=4,'expert_1'=2,'tile_0'=4,'tile_1'=4] {'expert_0'}, use_global_device_ids=true, to_apply=%region_1.2 | all-reduce | flops 1 | bytes 8 | tf_op jit(solution)/shard_map/psum | solution.py:19
  95.7 3.1 %psum.29 = f32[]{:T(128)} all-reduce(f32[]{:T(128)} %psum.28), channel_id=1, replica_groups=mesh['expert_0'=4,'expert_1'=2,'tile_0'=4,'tile_1'=4] {'expert_1'}, use_global_device_ids=true, to_apply=%region_2.3 | all-reduce | flops 1 | bytes 8 | tf_op jit(solution)/shard_map/psum | solution.py:19
  98.8 9.8 %psum.30 = f32[]{:T(128)} all-reduce(f32[]{:T(128)} %psum.29), channel_id=1, replica_groups=mesh['expert_0'=4,'expert_1'=2,'tile_0'=4,'tile_1'=4] {'tile_0'}, use_global_device_ids=true, to_apply=%region_3.4 | all-reduce | flops 1 | bytes 8 | tf_op jit(solution)/shard_map/psum | solution.py:19
  108.6 24.2 %psum.31 = f32[]{:T(128)} all-reduce(f32[]{:T(128)} %psum.30), channel_id=1, replica_groups=mesh['expert_0'=4,'expert_1'=2,'tile_0'=4,'tile_1'=4] {'tile_1'}, use_global_device_ids=true, to_apply=%region_4.5 | all-reduce | flops 1 | bytes 8 | tf_op jit(solution)/shard_map/psum | solution.py:19
  133.5 7.8 %fusion.4 = (f32[1,2048,512]{2,1,0:T(8,128)S(1)}, f32[1,2048,512]{2,1,0:T(8,128)S(1)}) fusion(f32[1,2048,512]{2,1,0:T(8,128)} %param.9, f32[]{:T(128)S(6)} %div.10, f32[1,2048,512]{2,1,0:T(8,128)} %param.8, bf16[1,1024,512]{2,1,0:T(8,128)(2,1)S(1)} %copy-done, bf16[2048,512]{1,0:T(8,128)(2,1)} %bitcast.4, bf16[2048,512]{1,0:T(8,128)(2,1)} %bitcast.2, pred[]{:T(512)S(6)} %eq.9), kind=kOutput, calls=%fused_computation.8 | convolution fusion | flops 2174746624 | bytes 22020100 | tf_op jit(solution)/shard_map/edk,ekj->edj/dot_general | solution.py:59
  141.4 0.0 copy-start.4
  141.4 0.0 copy-start.5
  141.4 2.8 %convolution_bitcast_fusion = f32[1,2048,1024]{2,1,0:T(8,128)S(1)} fusion(f32[1,2048,512]{2,1,0:T(8,128)S(1)} %get-tuple-element.4, f32[1,2048,512]{2,1,0:T(8,128)S(1)} %get-tuple-element.3, bf16[1,1024,512]{2,1,0:T(8,128)(2,1)S(1)} %copy-done), kind=kOutput, calls=%fused_computation.3 | convolution fusion | flops 2150629376 | bytes 17825792 | tf_op jit(solution)/shard_map/edj,ekj->edk/dot_general | solution.py:66
  144.2 0.5 copy-done.5
  144.7 0.4 select_convert_fusion
  145.1 0.3 collective-permute-start.1
  145.4 44.3 %collective-permute-done.1 = bf16[1,2048,512]{2,1,0:T(8,128)(2,1)S(1)} collective-permute-done((bf16[1,2048,512]{2,1,0:T(8,128)(2,1)S(1)}, bf16[1,2048,512]{2,1,0:T(8,128)(2,1)S(1)}, u32[]{:S(2)}, u32[]{:S(2)}) %collective-permute-start.1) | collective-permute-done | bytes 2097184 | tf_op jit(solution)/shard_map/ppermute | solution.py:26
  189.7 1.2 add_convert_fusion
  190.9 4.3 %convolution_bitcast_fusion.1 = f32[2,1024,512]{1,2,0:T(8,128)} fusion(bf16[2,1024,512]{2,1,0:T(8,128)(2,1)S(1)} %bitcast.36, bf16[1024,2,1024]{0,2,1:T(8,128)(2,1)S(1)} %bitcast.35), kind=kOutput, calls=%fused_computation.22 | convolution fusion | flops 2147483648 | bytes 10485760 | tf_op jit(solution)/shard_map/ekbi,ebiw->ebkw/dot_general | solution.py:81
  195.2 5.6 %copy.15 = f32[2,1024,512]{2,1,0:T(8,128)} copy(f32[2,1024,512]{1,2,0:T(8,128)} %convolution_bitcast_fusion.1) | data formatting | bytes 8388608 | tf_op jit(solution)/shard_map/ekbi,ebiw->ebkw/dot_general | solution.py:81
  200.8 4.3 %fusion.2 = bf16[1,2048,512]{2,1,0:T(8,128)(2,1)} fusion(bf16[1,2048,512]{2,1,0:T(8,128)(2,1)S(1)} %copy-done.3, f32[1,2048,512]{2,1,0:T(8,128)} %bitcast.33), kind=kLoop, calls=%fused_computation.6 | loop fusion | flops 6291456 | bytes 8388608 | tf_op jit(solution)/shard_map/convert_element_type | solution.py:85
  (9 shorter events, 0.0 us)
Async XLA Ops:
  7.2 126.4 %copy-start = (bf16[1,1024,512]{2,1,0:T(8,128)(2,1)S(1)}, bf16[1,1024,512]{2,1,0:T(8,128)(2,1)}, u32[]{:S(2)}) copy-start(bf16[1,1024,512]{2,1,0:T(8,128)(2,1)} %param.11) | copy-start | bytes 3145732
  7.2 62.4 %all-gather.2.cloned.1.call-start = ((), (), s32[]{:S(2)}) async-start(), calls=%async_computation | async-start | bytes 4456448 | tf_op jit(solution)/shard_map/all_gather | solution.py:49
  7.9 68.1 %copy-start.2 = (bf16[1,2048,512]{2,1,0:T(8,128)(2,1)S(1)}, bf16[1,2048,512]{2,1,0:T(8,128)(2,1)}, u32[]{:S(2)}) copy-start(bf16[1,2048,512]{2,1,0:T(8,128)(2,1)} %param.7) | copy-start | bytes 6291460
  81.8 51.7 %collective-permute-start = (bf16[1,2048,512]{2,1,0:T(8,128)(2,1)}, bf16[1,2048,512]{2,1,0:T(8,128)(2,1)}, u32[]{:S(2)}, u32[]{:S(2)}) collective-permute-start(bf16[1,2048,512]{2,1,0:T(8,128)(2,1)} %bitcast.3), channel_id=1, source_target_pairs={{0,1},{1,0},{2,3},{3,2},{4,5},{5,4},{6,7},{7,6},{8,9},{9,8},{10,11... | collective-permute-start | bytes 6291464 | tf_op jit(solution)/shard_map/ppermute | solution.py:26
  141.4 2.8 %copy-start.4 = (f32[1,2048,512]{2,1,0:T(8,128)}, f32[1,2048,512]{2,1,0:T(8,128)S(1)}, u32[]{:S(2)}) copy-start(f32[1,2048,512]{2,1,0:T(8,128)S(1)} %get-tuple-element.3) | copy-start | bytes 12582916
  141.4 3.4 %copy-start.5 = (f32[1,2048,512]{2,1,0:T(8,128)}, f32[1,2048,512]{2,1,0:T(8,128)S(1)}, u32[]{:S(2)}) copy-start(f32[1,2048,512]{2,1,0:T(8,128)S(1)} %get-tuple-element.4) | copy-start | bytes 12582916
  145.1 45.8 %copy-start.1 = (bf16[1,1024,2048]{1,2,0:T(8,128)(2,1)S(1)}, bf16[1,1024,2048]{1,2,0:T(8,128)(2,1)}, u32[]{:S(2)}) copy-start(bf16[1,1024,2048]{1,2,0:T(8,128)(2,1)} %copy.12) | copy-start | bytes 12582916
  145.1 44.5 %collective-permute-start.1 = (bf16[1,2048,512]{2,1,0:T(8,128)(2,1)S(1)}, bf16[1,2048,512]{2,1,0:T(8,128)(2,1)S(1)}, u32[]{:S(2)}, u32[]{:S(2)}) collective-permute-start(bf16[1,2048,512]{2,1,0:T(8,128)(2,1)S(1)} %select_convert_fusion), channel_id=1, source_target_pairs={{0,1},{1,0},{2,3},{3,2},{4,5},{5,4},{6,7},{7,6},{8,9},{9,8},{10,11... | collective-permute-start | bytes 6291464 | tf_op jit(solution)/shard_map/ppermute | solution.py:26
  195.2 5.6 %copy-start.3 = (bf16[1,2048,512]{2,1,0:T(8,128)(2,1)S(1)}, bf16[1,2048,512]{2,1,0:T(8,128)(2,1)}, u32[]{:S(2)}) copy-start(bf16[1,2048,512]{2,1,0:T(8,128)(2,1)} %param.6) | copy-start | bytes 6291460
Sparse Core Ops, SparseCore 0:
  10.1 59.4 all-gather.1
where the time goes:
time: 212 us
  waiting for transfers between devices  107 us (50%)
  blocking collectives  48.1 us (23%)
  matrix products  20.8 us (10%)
  between operations  14.9 us (7%)
  local copies, waits for them, and re-layouts  12.5 us (6%)
  other arithmetic  7.61 us (4%)
    all_gather x1, waiting for transfers between devices, on_device(): whole_left = lax.all_gather(left_basis, TILE, axis=2, tiled=True)  61.7 us
    psum x4, blocking collectives, one_axis_at_a_time(): value = lax.psum(value, axis)  48.1 us
    ppermute x2, waiting for transfers between devices, swapped(): return lax.ppermute(value, axis, pairs)  44.3 us
    dot_general x1, matrix products, on_device(): jnp.einsum('edk,ekj->edj', left_block, right_basis, preferred_element_typ...  7.82 us
    all_gather x1, local copies, waits for them, and re-layouts, on_device(): whole_left = lax.all_gather(left_basis, TILE, axis=2, tiled=True)  6.4 us
    dot_general x1, matrix products, on_device(): jnp.einsum('ekbi,ebkw->ebiw', left4, grad4, preferred_element_type=jnp.fl...  5.83 us
    dot_general x1, local copies, waits for them, and re-layouts, on_device(): jnp.einsum('ekbi,ebiw->ebkw', left4, back4, preferred_element_type=jnp.fl...  5.56 us
    convert_element_type x1, other arithmetic, on_device(): (weight32 - learn_rate * (back + decay_rate * weight32)).astype(jnp.bfloa...  4.33 us
  transfers between devices with their start and end apart: 3, of which 2 were waited for; matrix products, arithmetic and copies ran while one was open for 1% of the time, Pallas kernels for 0%

commit v1 on v0

--- a/solution.py
+++ b/solution.py
@@ -46,7 +46,9 @@
     total = one_axis_at_a_time(local_total, EXPERT_TILE)
     count = experts * lax.axis_size(EXPERT) * rows * width * lax.axis_size(TILE)
     clip = 1.0 / jnp.maximum(1.0, jnp.sqrt(total / count))
-    whole_left = lax.all_gather(left_basis, TILE, axis=2, tiled=True)
+    whole_left = jnp.concatenate(
+        lax.all_to_all(jnp.stack([left_basis] * lax.axis_size(TILE)), TILE, 0, 0), axis=2
+    )
     left4 = whole_left.reshape(experts, block, left_count, block)
     grad4 = grad.reshape(experts, left_count, block, width)
     rotated_left = jnp.einsum("ekbi,ebkw->ebiw", left4, grad4, preferred_element_type=jnp.float32)

time: 212 us -> 184 us (0.87)
  waiting for transfers between devices: 107 us -> 43.3 us
  blocking collectives: 48.1 us -> 106 us
  between operations: 14.9 us -> 1.49 us
  matrix products: 20.8 us -> 15.9 us
  local copies, waits for them, and re-layouts: 12.5 us -> 7.84 us
    all_gather x1 -> x0, waiting for transfers between devices: 61.7 us -> none  [on_device(): whole_left = lax.all_gather(left_basis, TILE, axis=2, tiled=True)]
    all_to_all x0 -> x1, blocking collectives: none -> 58.9 us  [on_device(): lax.all_to_all(jnp.stack([left_basis] * lax.axis_size(TILE)), TILE, 0, 0)]
    all_gather x1 -> x0, local copies, waits for them, and re-layouts: 6.4 us -> none  [on_device(): whole_left = lax.all_gather(left_basis, TILE, axis=2, tiled=True)]
    dot_general x1, matrix products: 5.83 us -> 2.33 us  [on_device(): jnp.einsum('ekbi,ebkw->ebiw', left4, grad4, preferred_element_type=jnp.fl...]
  transfers between devices with their start and end apart: 3 -> 2, of which waited for: 2 -> 1; matrix products, arithmetic and copies ran while one was open for 1% -> 1% of each run, Pallas kernels for 0% -> 0%
where the time goes in v1:
time: 184 us
  blocking collectives  106 us (58%)
  waiting for transfers between devices  43.3 us (24%)
  matrix products  15.9 us (9%)
  local copies, waits for them, and re-layouts  7.84 us (4%)
  other arithmetic  7.61 us (4%)
  starting transfers between devices  2.1 us (1%)
    all_to_all x1, blocking collectives, on_device(): lax.all_to_all(jnp.stack([left_basis] * lax.axis_size(TILE)), TILE, 0, 0)  58.9 us
    psum x4, blocking collectives, one_axis_at_a_time(): value = lax.psum(value, axis)  46.8 us
    ppermute x2, waiting for transfers between devices, swapped(): return lax.ppermute(value, axis, pairs)  43.3 us
    dot_general x1, matrix products, on_device(): jnp.einsum('edk,ekj->edj', left_block, right_basis, preferred_element_typ...  6.46 us
    dot_general x1, local copies, waits for them, and re-layouts, on_device(): jnp.einsum('ekbi,ebiw->ebkw', left4, back4, preferred_element_type=jnp.fl...  5.56 us
    convert_element_type x1, other arithmetic, on_device(): (weight32 - learn_rate * (back + decay_rate * weight32)).astype(jnp.bfloa...  4.33 us
    dot_general x1, matrix products, on_device(): jnp.einsum('ekbi,ebiw->ebkw', left4, back4, preferred_element_type=jnp.fl...  4.3 us
  transfers between devices with their start and end apart: 2, of which 1 were waited for; matrix products, arithmetic and copies ran while one was open for 1% of the time, Pallas kernels for 0%

profile of v1, /device:TPU:0, one launch (start us, length us, event | category | flops | bytes accessed | tf_op | source)
XLA Modules:
  0.0 184.0 jit_solution(4391200850364214361)
XLA Ops:
  0.6 0.0 copy-start
  0.6 1.2 copy.16
  1.8 0.5 stack.2
  2.4 0.0 copy-start.3
  2.4 58.9 %all_to_all.5 = bf16[16,1,1024,128]{2,3,1,0:T(8,128)(2,1)S(1)} all-to-all(bf16[16,1,1024,128]{2,3,1,0:T(8,128)(2,1)S(1)} %stack.2), channel_id=1, replica_groups=mesh['expert_0'=4,'expert_1'=2,'tile_0'=4,'tile_1'=4] {'tile_0','tile_1'}, dimensions={0} | all-to-all | bytes 8388608 | tf_op jit(solution)/shard_map/all_to_all | solution.py:50
  61.3 2.3 %convolution_convert_fusion = bf16[2,1024,512]{2,1,0:T(8,128)(2,1)S(1)} fusion(bf16[1024,2,1024]{0,2,1:T(8,128)(2,1)S(1)} %bitcast.37, bf16[2,1024,512]{2,1,0:T(8,128)(2,1)S(1)} %bitcast.40), kind=kOutput, calls=%fused_computation.24 | convolution fusion | flops 2148532224 | bytes 8388608 | tf_op jit(solution)/shard_map/ekbi,ebkw->ebiw/dot_general | solution.py:54
  63.7 0.6 collective-permute-start
  64.3 1.7 multiply_reduce_fusion
  66.0 11.1 %psum.28 = f32[]{:T(128)} all-reduce(f32[]{:T(128)} %multiply_reduce_fusion), channel_id=1, replica_groups=mesh['expert_0'=4,'expert_1'=2,'tile_0'=4,'tile_1'=4] {'expert_0'}, use_global_device_ids=true, to_apply=%region_1.2 | all-reduce | flops 1 | bytes 8 | tf_op jit(solution)/shard_map/psum | solution.py:19
  77.1 3.1 %psum.29 = f32[]{:T(128)} all-reduce(f32[]{:T(128)} %psum.28), channel_id=1, replica_groups=mesh['expert_0'=4,'expert_1'=2,'tile_0'=4,'tile_1'=4] {'expert_1'}, use_global_device_ids=true, to_apply=%region_2.3 | all-reduce | flops 1 | bytes 8 | tf_op jit(solution)/shard_map/psum | solution.py:19
  80.2 9.2 %psum.30 = f32[]{:T(128)} all-reduce(f32[]{:T(128)} %psum.29), channel_id=1, replica_groups=mesh['expert_0'=4,'expert_1'=2,'tile_0'=4,'tile_1'=4] {'tile_0'}, use_global_device_ids=true, to_apply=%region_3.4 | all-reduce | flops 1 | bytes 8 | tf_op jit(solution)/shard_map/psum | solution.py:19
  89.3 23.5 %psum.31 = f32[]{:T(128)} all-reduce(f32[]{:T(128)} %psum.30), channel_id=1, replica_groups=mesh['expert_0'=4,'expert_1'=2,'tile_0'=4,'tile_1'=4] {'tile_1'}, use_global_device_ids=true, to_apply=%region_4.5 | all-reduce | flops 1 | bytes 8 | tf_op jit(solution)/shard_map/psum | solution.py:19
  113.6 6.5 %fusion.4 = (f32[1,2048,512]{2,1,0:T(8,128)S(1)}, f32[1,2048,512]{2,1,0:T(8,128)S(1)}) fusion(f32[1,2048,512]{2,1,0:T(8,128)} %param.9, f32[]{:T(128)S(6)} %div.10, f32[1,2048,512]{2,1,0:T(8,128)} %param.8, bf16[1,1024,512]{2,1,0:T(8,128)(2,1)S(1)} %copy-done, bf16[2048,512]{1,0:T(8,128)(2,1)} %bitcast.6, bf16[2048,512]{1,0:T(8,128)(2,1)S(1)} %bitcast.43, ...), kind=kOutput, calls=%fused_computation.8 | convolution fusion | flops 2174746624 | bytes 22020100 | tf_op jit(solution)/shard_map/edk,ekj->edj/dot_general | solution.py:61
  120.0 0.0 copy-start.5
  120.0 0.0 copy-start.6
  120.0 2.8 %convolution_bitcast_fusion = f32[1,2048,1024]{2,1,0:T(8,128)S(1)} fusion(f32[1,2048,512]{2,1,0:T(8,128)S(1)} %get-tuple-element.4, f32[1,2048,512]{2,1,0:T(8,128)S(1)} %get-tuple-element.3, bf16[1,1024,512]{2,1,0:T(8,128)(2,1)S(1)} %copy-done), kind=kOutput, calls=%fused_computation.3 | convolution fusion | flops 2150629376 | bytes 17825792 | tf_op jit(solution)/shard_map/edj,ekj->edk/dot_general | solution.py:68
  122.9 0.5 copy-done.6
  123.4 0.4 select_convert_fusion
  123.8 1.5 collective-permute-start.1
  125.3 43.3 %collective-permute-done.1 = bf16[1,2048,512]{2,1,0:T(8,128)(2,1)S(1)} collective-permute-done((bf16[1,2048,512]{2,1,0:T(8,128)(2,1)S(1)}, bf16[1,2048,512]{2,1,0:T(8,128)(2,1)S(1)}, u32[]{:S(2)}, u32[]{:S(2)}) %collective-permute-start.1) | collective-permute-done | bytes 2097184 | tf_op jit(solution)/shard_map/ppermute | solution.py:26
  168.6 1.2 add_convert_fusion
  169.8 4.3 %convolution_bitcast_fusion.1 = f32[2,1024,512]{1,2,0:T(8,128)} fusion(bf16[2,1024,512]{2,1,0:T(8,128)(2,1)S(1)} %bitcast.39, bf16[1024,2,1024]{0,2,1:T(8,128)(2,1)S(1)} %bitcast.38), kind=kOutput, calls=%fused_computation.22 | convolution fusion | flops 2147483648 | bytes 10485760 | tf_op jit(solution)/shard_map/ekbi,ebiw->ebkw/dot_general | solution.py:83
  174.1 5.6 %copy.19 = f32[2,1024,512]{2,1,0:T(8,128)} copy(f32[2,1024,512]{1,2,0:T(8,128)} %convolution_bitcast_fusion.1) | data formatting | bytes 8388608 | tf_op jit(solution)/shard_map/ekbi,ebiw->ebkw/dot_general | solution.py:83
  179.7 4.3 %fusion.2 = bf16[1,2048,512]{2,1,0:T(8,128)(2,1)} fusion(bf16[1,2048,512]{2,1,0:T(8,128)(2,1)S(1)} %copy-done.4, f32[1,2048,512]{2,1,0:T(8,128)} %bitcast.36), kind=kLoop, calls=%fused_computation.6 | loop fusion | flops 6291456 | bytes 8388608 | tf_op jit(solution)/shard_map/convert_element_type | solution.py:87
  (10 shorter events, 0.0 us)
Async XLA Ops:
  0.6 112.9 %copy-start = (bf16[1,1024,512]{2,1,0:T(8,128)(2,1)S(1)}, bf16[1,1024,512]{2,1,0:T(8,128)(2,1)}, u32[]{:S(2)}) copy-start(bf16[1,1024,512]{2,1,0:T(8,128)(2,1)} %param.11) | copy-start | bytes 3145732
  2.4 59.0 %copy-start.3 = (bf16[1,2048,512]{2,1,0:T(8,128)(2,1)S(1)}, bf16[1,2048,512]{2,1,0:T(8,128)(2,1)}, u32[]{:S(2)}) copy-start(bf16[1,2048,512]{2,1,0:T(8,128)(2,1)} %param.7) | copy-start | bytes 6291460
  61.3 2.3 %copy-start.1 = (bf16[16,1,1024,128]{2,3,1,0:T(8,128)(2,1)}, bf16[16,1,1024,128]{2,3,1,0:T(8,128)(2,1)S(1)}, u32[]{:S(2)}) copy-start(bf16[16,1,1024,128]{2,3,1,0:T(8,128)(2,1)S(1)} %all_to_all.5) | copy-start | bytes 12582916
  63.7 49.9 %collective-permute-start = (bf16[1,2048,512]{2,1,0:T(8,128)(2,1)S(1)}, bf16[1,2048,512]{2,1,0:T(8,128)(2,1)}, u32[]{:S(2)}, u32[]{:S(2)}) collective-permute-start(bf16[1,2048,512]{2,1,0:T(8,128)(2,1)S(1)} %bitcast.42), channel_id=1, source_target_pairs={{0,1},{1,0},{2,3},{3,2},{4,5},{5,4},{6,7},{7,6},{8,9},{9,8},{10,11... | collective-permute-start | bytes 6291464 | tf_op jit(solution)/shard_map/ppermute | solution.py:26
  120.0 2.8 %copy-start.5 = (f32[1,2048,512]{2,1,0:T(8,128)}, f32[1,2048,512]{2,1,0:T(8,128)S(1)}, u32[]{:S(2)}) copy-start(f32[1,2048,512]{2,1,0:T(8,128)S(1)} %get-tuple-element.3) | copy-start | bytes 12582916
  120.0 3.4 %copy-start.6 = (f32[1,2048,512]{2,1,0:T(8,128)}, f32[1,2048,512]{2,1,0:T(8,128)S(1)}, u32[]{:S(2)}) copy-start(f32[1,2048,512]{2,1,0:T(8,128)S(1)} %get-tuple-element.4) | copy-start | bytes 12582916
  123.8 46.0 %copy-start.2 = (bf16[16,1,1024,128]{2,3,1,0:T(8,128)(2,1)S(1)}, bf16[16,1,1024,128]{2,3,1,0:T(8,128)(2,1)}, u32[]{:S(2)}) copy-start(bf16[16,1,1024,128]{2,3,1,0:T(8,128)(2,1)} %copy-done.1) | copy-start | bytes 12582916
  123.8 44.8 %collective-permute-start.1 = (bf16[1,2048,512]{2,1,0:T(8,128)(2,1)S(1)}, bf16[1,2048,512]{2,1,0:T(8,128)(2,1)S(1)}, u32[]{:S(2)}, u32[]{:S(2)}) collective-permute-start(bf16[1,2048,512]{2,1,0:T(8,128)(2,1)S(1)} %select_convert_fusion), channel_id=1, source_target_pairs={{0,1},{1,0},{2,3},{3,2},{4,5},{5,4},{6,7},{7,6},{8,9},{9,8},{10,11... | collective-permute-start | bytes 6291464 | tf_op jit(solution)/shard_map/ppermute | solution.py:26
  174.1 5.6 %copy-start.4 = (bf16[1,2048,512]{2,1,0:T(8,128)(2,1)S(1)}, bf16[1,2048,512]{2,1,0:T(8,128)(2,1)}, u32[]{:S(2)}) copy-start(bf16[1,2048,512]{2,1,0:T(8,128)(2,1)} %param.6) | copy-start | bytes 6291460
